TPU v7x, 32 devices: a whole 2x2x4 slice. The times are simulated.
32 devices in a mesh: ez: 4 (over z), ey: 2 (over y), ex: 4 (over x, core).
Axes of the slice: x: 2, y: 2, z: 4, core: 2. Of those that a mesh axis runs over, the one named last changes fastest.
Arguments:
- tokens: bfloat16 [8192, 2560], P(('ez', 'ey', 'ex'))
- expert_ids: int32 [8192, 6], P(('ez', 'ey', 'ex'))
- gate_weights: float32 [8192, 6], P(('ez', 'ey', 'ex'))
- w_gate: bfloat16 [64, 2560, 1536], P(('ez', 'ey', 'ex'))
- w_up: bfloat16 [64, 2560, 1536], P(('ez', 'ey', 'ex'))
- w_down: bfloat16 [64, 1536, 2560], P(('ez', 'ey', 'ex'))
Outputs:
- output: bfloat16 [8192, 2560], P(('ez', 'ey', 'ex'))
All inputs are finite; a program needn't handle non-finite values.
Results may differ from a plain program's by a relative error of at most 0.00615969.
Values are sent between devices in bfloat16 or wider.
A program may use at most 1 GiB of HBM per device.

v0:
```python
import math
import jax
import jax.numpy as jnp
from jax import lax
from jax.sharding import PartitionSpec as P


def pack_rows(chosen, gate_vals, per_expert):
    row_rank = jnp.cumsum(chosen.astype(jnp.int32), axis=0) - 1
    slot_idx = jnp.where(chosen, row_rank, per_expert)
    row_idx = jnp.broadcast_to(jnp.arange(chosen.shape[0])[:, None], chosen.shape)
    exp_idx = jnp.broadcast_to(jnp.arange(chosen.shape[1])[None, :], chosen.shape)
    pick_rows = jnp.zeros((chosen.shape[1], per_expert), jnp.int32).at[exp_idx, slot_idx].set(row_idx, mode="drop")
    pick_gates = jnp.zeros((chosen.shape[1], per_expert), jnp.float32).at[exp_idx, slot_idx].set(gate_vals, mode="drop")
    return pick_rows, pick_gates


def expert_ffn(x_pack, w_gate, w_up, w_down, pick_gates):
    gate_act = jnp.einsum("lch,lhf->lcf", x_pack, w_gate, preferred_element_type=jnp.float32)
    up_act = jnp.einsum("lch,lhf->lcf", x_pack, w_up, preferred_element_type=jnp.float32)
    hidden_act = (jax.nn.silu(gate_act) * up_act).astype(jnp.bfloat16)
    expert_out = jnp.einsum("lcf,lfh->lch", hidden_act, w_down, preferred_element_type=jnp.float32)
    return expert_out * pick_gates[:, :, None]


def solution(mesh):
    ep_axes = tuple(mesh.axis_names)
    num_devices = math.prod(mesh.shape[axis_name] for axis_name in ep_axes)
    row_spec = P(ep_axes, None)
    w_spec = P(ep_axes, None, None)

    def local_layer(tokens, expert_ids, gate_weights, w_gate, w_up, w_down):
        tok_dev, hidden = tokens.shape
        top_k = expert_ids.shape[1]
        local_experts = w_gate.shape[0]
        capacity = tok_dev * top_k // num_devices
        rows_recv = num_devices * capacity
        per_expert = rows_recv // local_experts
        dest_dev = expert_ids // local_experts
        dev_hit = jnp.any(dest_dev[:, :, None] == jnp.arange(num_devices)[None, None, :], axis=1)
        all_experts = jnp.arange(num_devices * local_experts)
        gate_dense = jnp.sum(jnp.where(expert_ids[:, :, None] == all_experts[None, None, :], gate_weights[:, :, None], 0.0), axis=1)
        gate_dense = gate_dense.reshape(tok_dev, num_devices, local_experts)
        slot_pos = jnp.cumsum(dev_hit.astype(jnp.int32), axis=0) - 1
        place_mask = dev_hit[:, :, None] & (slot_pos[:, :, None] == jnp.arange(capacity)[None, None, :])
        place_bf = place_mask.astype(jnp.bfloat16)
        send_rows = jnp.einsum("tdc,th->dch", place_bf, tokens, preferred_element_type=jnp.float32).astype(jnp.bfloat16)
        send_gates = jnp.sum(jnp.where(place_mask[:, :, :, None], gate_dense[:, :, None, :], 0.0), axis=0)
        recv_rows = lax.all_to_all(send_rows, ep_axes, 0, 0, tiled=True)
        recv_gates = lax.all_to_all(send_gates, ep_axes, 0, 0, tiled=True)
        flat_rows = recv_rows.reshape(rows_recv, hidden)
        flat_gates = recv_gates.reshape(rows_recv, local_experts)
        pick_rows, pick_gates = pack_rows(flat_gates > 0.0, flat_gates, per_expert)
        weighted = expert_ffn(flat_rows[pick_rows], w_gate, w_up, w_down, pick_gates)
        part_sum = jax.ops.segment_sum(weighted.reshape(-1, hidden), pick_rows.reshape(-1), num_segments=rows_recv)
        back_rows = part_sum.astype(jnp.bfloat16).reshape(num_devices, capacity, hidden)
        returned = lax.all_to_all(back_rows, ep_axes, 0, 0, tiled=True)
        moe_sum = jnp.einsum("tdc,dch->th", place_bf, returned, preferred_element_type=jnp.float32)
        return (tokens.astype(jnp.float32) + moe_sum).astype(jnp.bfloat16)

    return jax.shard_map(local_layer, mesh=mesh, in_specs=(row_spec, row_spec, row_spec, w_spec, w_spec, w_spec), out_specs=row_spec, check_vma=False)
```

profile of v0, /device:TPU:0, one launch (start us, length us, event | category | flops | bytes accessed | tf_op | source)
XLA Modules:
  0.0 499.3 jit_solution(13349808334063705440)
XLA Ops:
  0.0 0.7 add_select_fusion
  0.8 0.6 reduce-window.14
  1.7 0.8 select_reduce_fusion.1
  2.5 0.3 fusion.4
  2.8 1.1 select_reduce_fusion
  4.0 7.4 %all-to-all-start = ((f32[32,48,2]{1,2,0:T(2,128)}), f32[32,48,2]{1,2,0:T(2,128)S(1)}, u32[]{:S(2)}, u32[]{:S(2)}) async-start(f32[32,48,2]{1,2,0:T(2,128)} %select_reduce_fusion), calls=%async_computation | async-start | bytes 65536 | tf_op jit(solution)/shard_map/all_to_all | solution.py:50
  11.3 6.7 %convolution_convert_fusion = bf16[32,48,2560]{2,1,0:T(8,128)(2,1)} fusion(bf16[256,2560]{1,0:T(8,128)(2,1)} %param.6, s32[256,32]{0,1:T(8,128)S(1)} %bitcast_bitcast_fusion, pred[256,32]{0,1:T(8,128)(4,1)S(1)} %fusion.6), kind=kOutput, calls=%fused_computation.8 | convolution fusion | flops 2017984512 | bytes 9216000 | tf_op jit(solution)/shard_map/tdc,th->dch/dot_general | solution.py:47
  18.0 0.4 all-to-all-done
  18.4 5.6 %all-to-all-start.1 = ((bf16[32,48,2560]{2,1,0:T(8,128)(2,1)}), bf16[32,48,2560]{2,1,0:T(8,128)(2,1)}, u32[]{:S(2)}, u32[]{:S(2)}) async-start(bf16[32,48,2560]{2,1,0:T(8,128)(2,1)} %convolution_convert_fusion), calls=%async_computation.1 | async-start | bytes 15728640 | tf_op jit(solution)/shard_map/all_to_all | solution.py:49
  24.1 0.4 reshape.96
  24.6 0.6 reduce-window.16
  25.9 0.4 reshape.102
  26.9 0.4 reshape.94
  27.3 11.8 %scatter_custom_fusion.2 = f32[1536]{0:T(1024)S(1)} fusion(s32[3072]{0:T(1024)S(1)} %reshape.94, f32[3072]{0:T(1024)S(1)} %reshape.102, f32[]{:T(128)} %constant.39.clone.1), kind=kCustom, calls=%fused_computation.46 | custom fusion | bytes 6148
  39.1 11.8 %scatter_custom_fusion.1 = s32[1536]{0:T(1024)S(1)} fusion(s32[3072]{0:T(1024)S(1)} %reshape.94, s32[3072]{0:T(1024)S(1)} %reshape.96, s32[]{:T(128)} %constant.20.clone.1), kind=kCustom, calls=%fused_computation.48 | custom fusion | bytes 6148 | tf_op jit(solution)/shard_map/broadcast_in_dim;reshape | solution.py:55
  50.9 137.6 %all-to-all-done.1 = bf16[32,48,2560]{2,1,0:T(8,128)(2,1)} async-done(((bf16[32,48,2560]{2,1,0:T(8,128)(2,1)}), bf16[32,48,2560]{2,1,0:T(8,128)(2,1)}, u32[]{:S(2)}, u32[]{:S(2)}) %all-to-all-start.1) | async-done | bytes 7864352 | tf_op jit(solution)/shard_map/all_to_all | solution.py:49
  188.5 19.5 %gather_fusion = bf16[1536,2560]{1,0:T(8,128)(2,1)} fusion(bf16[1536,2560]{1,0:T(8,128)(2,1)} %bitcast.6, s32[2048]{0:T(1024)S(1)} %pad_clamp_fusion), kind=kCustom, calls=%fused_computation | custom fusion | bytes 15734784 | tf_op jit(solution)/shard_map/gather | solution.py:54
  208.1 19.5 %fusion.17 = f32[2,768,1536]{2,1,0:T(8,128)} fusion(bf16[2,768,2560]{2,1,0:T(8,128)(2,1)} %bitcast.59, bf16[2,2560,1536]{2,1,0:T(8,128)(2,1)} %param.9), kind=kOutput, calls=%fused_computation.50 | convolution fusion | flops 12079595520 | bytes 33030144 | tf_op jit(solution)/shard_map/lch,lhf->lcf/dot_general | solution.py:19
  227.6 19.1 %multiply_convert_fusion = bf16[2,768,1536]{2,1,0:T(8,128)(2,1)} fusion(f32[2,768,1536]{2,1,0:T(8,128)} %fusion.17, bf16[2,768,2560]{2,1,0:T(8,128)(2,1)S(1)} %bitcast.60, bf16[2,2560,1536]{2,1,0:T(8,128)(2,1)} %param.10), kind=kOutput, calls=%fused_computation.5 | convolution fusion | flops 12093751296 | bytes 37748736 | tf_op jit(solution)/shard_map/lch,lhf->lcf/dot_general | solution.py:20
  246.7 20.5 %convolution_multiply_fusion = f32[2,768,2560]{2,1,0:T(8,128)} fusion(bf16[2,768,1536]{2,1,0:T(8,128)(2,1)} %multiply_convert_fusion, bf16[2,1536,2560]{2,1,0:T(8,128)(2,1)} %param.11, f32[2,768]{1,0:T(2,128)S(1)} %reshape.74), kind=kOutput, calls=%fused_computation.4 | convolution fusion | flops 12083527680 | bytes 36182016 | tf_op jit(solution)/shard_map/lcf,lfh->lch/dot_general | solution.py:22
  267.2 31.7 %scatter_custom_fusion = f32[1536,2560]{1,0:T(8,128)} fusion(s32[1536]{0:T(1024)S(1)} %scatter_custom_fusion.1, f32[1536,2560]{1,0:T(8,128)} %bitcast.62, f32[]{:T(128)} %constant.39.clone.1), kind=kCustom, calls=%fused_computation.6 | custom fusion | flops 3932160 | bytes 15729152 | tf_op jit(solution)/shard_map/scatter-add | solution.py:55
  299.0 9.5 %convert_element_type.26 = bf16[1536,2560]{1,0:T(8,128)(2,1)} convert(f32[1536,2560]{1,0:T(8,128)} %scatter_custom_fusion) | non-fusion elementwise | flops 3932160 | bytes 23592960 | tf_op jit(solution)/shard_map/convert_element_type | solution.py:56
  308.5 187.4 %all_to_all.15 = bf16[32,48,2560]{2,1,0:T(8,128)(2,1)S(1)} all-to-all(bf16[32,48,2560]{2,1,0:T(8,128)(2,1)} %bitcast.58), channel_id=1, replica_groups=mesh['ez'=4,'ey'=2,'ex'=4] {'ez','ey','ex'}, dimensions={0} | all-to-all | bytes 15728640 | tf_op jit(solution)/shard_map/all_to_all | solution.py:57
  495.9 3.3 fusion.3
  (35 shorter events, 1.9 us)
Async XLA Ops:
  4.0 14.5 %all-to-all-start = ((f32[32,48,2]{1,2,0:T(2,128)}), f32[32,48,2]{1,2,0:T(2,128)S(1)}, u32[]{:S(2)}, u32[]{:S(2)}) async-start(f32[32,48,2]{1,2,0:T(2,128)} %select_reduce_fusion), calls=%async_computation | async-start | bytes 65536 | tf_op jit(solution)/shard_map/all_to_all | solution.py:50
  18.0 8.3 %copy-start.3 = (s32[2]{0:T(128)S(1)}, s32[2]{0:T(128)}, u32[]{:S(2)}) copy-start(s32[2]{0:T(128)} %constant.46) | copy-start | bytes 28
  18.0 8.4 %copy-start.2 = (s32[2]{0:T(128)S(1)}, s32[2]{0:T(128)}, u32[]{:S(2)}) copy-start(s32[2]{0:T(128)} %constant.49) | copy-start | bytes 28
  18.4 170.1 %all-to-all-start.1 = ((bf16[32,48,2560]{2,1,0:T(8,128)(2,1)}), bf16[32,48,2560]{2,1,0:T(8,128)(2,1)}, u32[]{:S(2)}, u32[]{:S(2)}) async-start(bf16[32,48,2560]{2,1,0:T(8,128)(2,1)} %convolution_convert_fusion), calls=%async_computation.1 | async-start | bytes 15728640 | tf_op jit(solution)/shard_map/all_to_all | solution.py:49
  208.1 19.6 %copy-start = (bf16[1536,2560]{1,0:T(8,128)(2,1)S(1)}, bf16[1536,2560]{1,0:T(8,128)(2,1)}, u32[]{:S(2)}) copy-start(bf16[1536,2560]{1,0:T(8,128)(2,1)} %gather_fusion) | copy-start | bytes 23592964
  308.5 187.5 %copy-start.1 = (bf16[256,2560]{1,0:T(8,128)(2,1)S(1)}, bf16[256,2560]{1,0:T(8,128)(2,1)}, u32[]{:S(2)}) copy-start(bf16[256,2560]{1,0:T(8,128)(2,1)} %param.6) | copy-start | bytes 3932164
where the time goes:
time: 500 us; the launch traced here: 499 us
  blocking collectives  187 us (37%)
  waiting for transfers between devices  138 us (28%)
  matrix products  69.2 us (14%)
  other arithmetic  46.1 us (9%)
  local copies, waits for them, and re-layouts  45.5 us (9%)
  starting transfers between devices  12.9 us (3%)
    all_to_all x1, blocking collectives, local_layer(): returned = lax.all_to_all(back_rows, ep_axes, 0, 0, tiled=True)  187 us
    all_to_all x1, waiting for transfers between devices, local_layer(): recv_rows = lax.all_to_all(send_rows, ep_axes, 0, 0, tiled=True)  138 us
    scatter-add x1, other arithmetic, local_layer(): jax.ops.segment_sum(weighted.reshape(-1, hidden), pick_rows.reshape(-1),...  31.7 us
    dot_general x1, matrix products, expert_ffn(): jnp.einsum('lcf,lfh->lch', hidden_act, w_down, preferred_element_type=jnp...  20.5 us
    dot_general x1, matrix products, expert_ffn(): jnp.einsum('lch,lhf->lcf', x_pack, w_gate, preferred_element_type=jnp.flo...  19.5 us
    gather x1, local copies, waits for them, and re-layouts, local_layer(): flat_rows[pick_rows]  19.5 us
    dot_general x1, matrix products, expert_ffn(): jnp.einsum('lch,lhf->lcf', x_pack, w_up, preferred_element_type=jnp.float32)  19.1 us
    unnamed x11, local copies, waits for them, and re-layouts  12.5 us
  transfers between devices with their start and end apart: 2, of which 2 were waited for; matrix products, arithmetic and copies ran while one was open for 7% of the time, Pallas kernels for 0%

commit v1 on v0

v1 whole, which is shorter than its diff:
```python
import functools
import math
import jax
import jax.numpy as jnp
from jax import lax
from jax.experimental import pallas as pl
from jax.experimental.pallas import tpu as pltpu
from jax.sharding import PartitionSpec as P

BF = jnp.bfloat16
F32 = jnp.float32
MESH = pl.DeviceIdType.MESH
TAIL = 128
PLANE = 8
ZED = 4
SLICES = 4


def layer_kernel(dims, x_ref, tail_ref, w1_ref, w3_ref, w2_ref, y_ref,
                 zbuf, send, recv, back, hid, zsend, zrecv, unpack, wa, wb,
                 x_sem, wa_sem, wb_sem, z_ssem, z_rsem, d_ssem, d_rsem,
                 b_ssem, b_rsem, s_ssem, s_rsem):
    tok, wide, ff, cap, ft, nt = dims
    rows = PLANE * cap
    full = wide + TAIL
    sw = wide // SLICES
    n_f, n_n = ff // ft, wide // nt
    z = lax.axis_index("ez")
    ey = lax.axis_index("ey")
    ex = lax.axis_index("ex")
    me = ey * 4 + ex
    mid = jnp.logical_and(z > 0, z < 3)
    end = jnp.logical_or(z < 1, z > 2)

    def peer(o):
        cy = ey if o < 4 else 1 - ey
        cx = (ex, ex + 1 - 2 * (ex % 2), (ex + 2) % 4, 3 - ex)[o % 4]
        return cy, cx

    def rows_of(q):
        return pl.ds(pl.multiple_of(q * cap, cap), cap)

    src_z = (z, z + 1 - 2 * (z % 2), 2 - z // 2, 3 - 3 * (z // 2))
    order = (6, 4, 2, 7, 5, 3, 1)

    barrier = pltpu.get_barrier_semaphore()
    for o in range(1, PLANE):
        cy, cx = peer(o)
        pl.semaphore_signal(barrier, inc=1, device_id=(z, cy, cx), device_id_type=MESH)

    @pl.when(z > 0)
    def _():
        pl.semaphore_signal(barrier, inc=1, device_id=(z - 1, ey, ex), device_id_type=MESH)

    @pl.when(z < 3)
    def _():
        pl.semaphore_signal(barrier, inc=1, device_id=(z + 1, ey, ex), device_id_type=MESH)

    own = pltpu.make_async_copy(x_ref, zbuf.at[z, :, pl.ds(0, wide)], x_sem.at[0])
    own.start()
    zbuf[z, :, wide:] = tail_ref[...]

    def a_copies(i):
        l, f, slot = i // n_f, i % n_f, i % 2
        cols = pl.ds(pl.multiple_of(f * ft, ft), ft)
        return [pltpu.make_async_copy(w.at[l, :, cols], wa.at[slot, j], wa_sem.at[slot, j])
                for j, w in enumerate((w1_ref, w3_ref))]

    def b_copies(n):
        slot = n % 2
        cols = pl.ds(pl.multiple_of(n * nt, nt), nt)
        return [pltpu.make_async_copy(w2_ref.at[l, :, cols], wb.at[slot, l], wb_sem.at[slot, l])
                for l in range(2)]

    for c in a_copies(0):
        c.start()
    own.wait()
    pl.semaphore_wait(barrier, PLANE - 1 + jnp.where(mid, 2, 1))

    def z_copy(block, target, i):
        return pltpu.make_async_remote_copy(
            src_ref=zbuf.at[block], dst_ref=zbuf.at[block],
            send_sem=z_ssem.at[i], recv_sem=z_rsem.at[block],
            device_id=(target, ey, ex), device_id_type=MESH)

    @pl.when(z > 0)
    def _():
        z_copy(z, z - 1, 0).start()

    @pl.when(z < 3)
    def _():
        z_copy(z, z + 1, 1).start()

    def fwd_copy(k):
        return z_copy(src_z[k], 3 - z if k == 1 else 3 * (z - 1), 1 + k)

    def z_wait(k):
        z_copy(src_z[k], z, 0).wait_recv()

    def d_copy(k, o):
        cy, cx = peer(o)
        return pltpu.make_async_remote_copy(
            src_ref=send.at[k, rows_of(cy * 4 + cx)], dst_ref=recv.at[k, rows_of(me)],
            send_sem=d_ssem.at[k, o], recv_sem=d_rsem.at[k, o],
            device_id=(z, cy, cx), device_id_type=MESH)

    def relay(k):
        b = src_z[k]
        tail = zbuf[b, :, wide:].astype(F32)
        lane = lax.broadcasted_iota(jnp.int32, (tok, TAIL), 1)
        want_dev = jnp.where(lane < PLANE, z * PLANE + lane, -2).astype(F32)
        want_exp = jnp.where(lane < 48, z * 16 + jnp.bitwise_and(lane, 15), -2).astype(F32)
        hit = jnp.zeros((tok, TAIL), F32)
        gates = jnp.zeros((tok, TAIL), F32)
        for j in range(6):
            hit = jnp.where(tail[:, j:j + 1] == want_dev, 1.0, hit)
            part = jnp.where(lane < 16, tail[:, 16 + j:17 + j],
                             jnp.where(lane < 32, tail[:, 24 + j:25 + j], tail[:, 32 + j:33 + j]))
            gates = jnp.where(tail[:, 8 + j:9 + j] == want_exp, part, gates)
        r_i = lax.broadcasted_iota(jnp.int32, (tok, tok), 0)
        c_i = lax.broadcasted_iota(jnp.int32, (tok, tok), 1)
        tri = jnp.where(c_i <= r_i, 1.0, 0.0).astype(BF)
        rank = jnp.dot(tri, hit.astype(BF), preferred_element_type=F32)
        pos = jnp.where(hit > 0.0, rank, 0.0).astype(BF)
        d_i = lax.broadcasted_iota(jnp.int32, (TAIL, rows), 0)
        s_i = lax.broadcasted_iota(jnp.int32, (TAIL, rows), 1)
        spread = jnp.where(jnp.logical_and(s_i >= d_i * cap, s_i < d_i * cap + cap), 1.0, 0.0).astype(BF)
        l_i = lax.broadcasted_iota(jnp.int32, (tok, rows), 1)
        slot_l = l_i + 1
        for q in range(1, PLANE):
            slot_l = slot_l - jnp.where(l_i >= q * cap, cap, 0)
        at_l = jnp.dot(pos, spread, preferred_element_type=F32)
        unpack[k] = jnp.where(at_l == slot_l.astype(F32), 1.0, 0.0).astype(BF)
        d_t = lax.broadcasted_iota(jnp.int32, (rows, TAIL), 1)
        s_t = lax.broadcasted_iota(jnp.int32, (rows, TAIL), 0)
        spread_t = jnp.where(jnp.logical_and(s_t >= d_t * cap, s_t < d_t * cap + cap), 1.0, 0.0).astype(BF)
        r_t = lax.broadcasted_iota(jnp.int32, (rows, tok), 0)
        slot_r = r_t + 1
        for q in range(1, PLANE):
            slot_r = slot_r - jnp.where(r_t >= q * cap, cap, 0)
        at_r = lax.dot_general(spread_t, pos, (((1,), (1,)), ((), ())), preferred_element_type=F32)
        pick = jnp.where(at_r == slot_r.astype(F32), 1.0, 0.0).astype(BF)
        for s in range(SLICES):
            cols = slice(s * sw, s * sw + sw)
            send[k, :, cols] = jnp.dot(pick, zbuf[b, :, cols], preferred_element_type=F32).astype(BF)
        send[k, :, wide:] = jnp.dot(pick, gates.astype(BF), preferred_element_type=F32).astype(BF)
        for o in order:
            d_copy(k, o).start()
        recv[k, rows_of(me), :] = send[k, rows_of(me), :]

    def service(k):
        z_wait(k)
        relay(k)

    def forward(k):
        @pl.when(mid)
        def _():
            fwd_copy(k).start()

    def arrive(k):
        for o in order:
            d_copy(k, o).wait_recv()

    def stage_a(k, l):
        def step(i, carry):
            @pl.when(i + 1 < 2 * n_f)
            def _():
                for c in a_copies(i + 1):
                    c.start()

            @pl.when(i + 1 == 2 * n_f)
            def _():
                for c in b_copies(0):
                    c.start()
            for c in a_copies(i):
                c.wait()
            slot = i % 2
            x = recv[k, :, :wide]
            a = jnp.dot(x, wa[slot, 0], preferred_element_type=F32)
            b = jnp.dot(x, wa[slot, 1], preferred_element_type=F32)
            cols = pl.ds(pl.multiple_of((i - l * n_f) * ft, ft), ft)
            hid[l, :, cols] = (jax.nn.silu(a) * b).astype(BF)
            return carry
        lax.fori_loop(l * n_f, (l + 1) * n_f, step, 0)

    def stage_b(k):
        tail = recv[k, :, wide:].astype(F32)
        lane = lax.broadcasted_iota(jnp.int32, (rows, TAIL), 1)
        gate = []
        for l in range(2):
            at = jnp.where(lane < 48, jnp.bitwise_and(lane, 15), -1) == me * 2 + l
            gate.append(jnp.sum(jnp.where(at, tail, 0.0), axis=1, keepdims=True))

        def step(n, carry):
            @pl.when(n + 1 < n_n)
            def _():
                for c in b_copies(n + 1):
                    c.start()
            if k < ZED - 1:
                @pl.when(n + 1 == n_n)
                def _():
                    for c in a_copies(0):
                        c.start()
            for c in b_copies(n):
                c.wait()
            slot = n % 2
            o0 = jnp.dot(hid[0], wb[slot, 0], preferred_element_type=F32)
            o1 = jnp.dot(hid[1], wb[slot, 1], preferred_element_type=F32)
            cols = pl.ds(pl.multiple_of(n * nt, nt), nt)
            recv[k, :, cols] = (gate[0] * o0 + gate[1] * o1).astype(BF)
            return carry
        lax.fori_loop(0, n_n, step, 0)

    def b_copy(k, o):
        cy, cx = peer(o)
        return pltpu.make_async_remote_copy(
            src_ref=recv.at[k, rows_of(cy * 4 + cx), pl.ds(0, wide)], dst_ref=back.at[k, rows_of(me)],
            send_sem=b_ssem.at[k, o], recv_sem=b_rsem.at[k, o],
            device_id=(z, cy, cx), device_id_type=MESH)

    def give_back(k):
        for o in order:
            b_copy(k, o).start()
        back[k, rows_of(me), :] = recv[k, rows_of(me), :wide]

    def back_wait(k):
        for o in order:
            b_copy(k, o).wait_recv()

    def s_copy(k, s):
        if k == 1:
            target, slot = src_z[1], jnp.where(z % 2 == 0, z + 1, 4)
        elif k == 2:
            target = z + 1 - 2 * (z // 2)
            slot = jnp.where(z < 2, 2, jnp.where(z == 2, 4, 1))
        else:
            target, slot = z + 1 - 2 * (z // 2), src_z[3]
        cols = pl.ds(s * sw, sw)
        return pltpu.make_async_remote_copy(
            src_ref=zsend.at[k - 1, :, cols], dst_ref=zrecv.at[slot, :, cols],
            send_sem=s_ssem.at[k - 1, s], recv_sem=s_rsem.at[slot, s],
            device_id=(target, ey, ex), device_id_type=MESH)

    def s_wait(slot, s):
        cols = pl.ds(s * sw, sw)
        pltpu.make_async_remote_copy(
            src_ref=zsend.at[0, :, cols], dst_ref=zrecv.at[slot, :, cols],
            send_sem=s_ssem.at[0, s], recv_sem=s_rsem.at[slot, s],
            device_id=(z, ey, ex), device_id_type=MESH).wait_recv()

    def partial(k, s):
        return jnp.dot(unpack[k], back[k, :, s * sw:s * sw + sw], preferred_element_type=F32)

    def finish_end(k):
        for s in range(SLICES):
            zsend[k - 1, :, s * sw:s * sw + sw] = partial(k, s).astype(BF)
            s_copy(k, s).start()

    def finish_mid(k):
        for s in range(SLICES):
            cols = slice(s * sw, s * sw + sw)
            s_wait(src_z[k], s)
            total = partial(k, s) + zrecv[src_z[k], :, cols].astype(F32)
            zsend[k - 1, :, cols] = total.astype(BF)
            s_copy(k, s).start()

    def finish(k):
        back_wait(k)
        pl.when(end)(lambda: finish_end(k))
        pl.when(mid)(lambda: finish_mid(k))

    relay(0)
    arrive(0)
    stage_a(0, 0)
    z_wait(1)
    forward(1)

    @pl.when(mid)
    def _():
        z_wait(2)
        fwd_copy(2).start()
    relay(1)
    stage_a(0, 1)
    stage_b(0)

    arrive(1)
    stage_a(1, 0)

    @pl.when(end)
    def _():
        z_wait(2)
    relay(2)

    @pl.when(mid)
    def _():
        z_wait(3)
        fwd_copy(3).start()
    stage_a(1, 1)
    stage_b(1)
    give_back(1)

    arrive(2)
    stage_a(2, 0)

    @pl.when(end)
    def _():
        z_wait(3)
    relay(3)
    stage_a(2, 1)
    stage_b(2)
    give_back(2)

    @pl.when(end)
    def _():
        back_wait(1)
        finish_end(1)
    arrive(3)
    stage_a(3, 0)
    stage_a(3, 1)
    stage_b(3)
    give_back(3)
    give_back(0)
    finish(2)
    finish(3)

    @pl.when(mid)
    def _():
        back_wait(1)
        finish_mid(1)
    back_wait(0)

    for s in range(SLICES):
        cols = slice(s * sw, s * sw + sw)

        @pl.when(z > 0)
        def _():
            s_wait(z, s)

        @pl.when(z < 3)
        def _():
            s_wait(4, s)
        total = zbuf[z, :, cols].astype(F32) + partial(0, s)

        @pl.when(z == 0)
        def _():
            y_ref[:, cols] = (total + zrecv[4, :, cols].astype(F32)).astype(BF)

        @pl.when(z == 3)
        def _():
            y_ref[:, cols] = (total + zrecv[3, :, cols].astype(F32)).astype(BF)

        @pl.when(mid)
        def _():
            both = zrecv[z, :, cols].astype(F32) + zrecv[4, :, cols].astype(F32)
            y_ref[:, cols] = (total + both).astype(BF)

    @pl.when(z > 0)
    def _():
        z_copy(z, z - 1, 0).wait_send()

    @pl.when(z < 3)
    def _():
        z_copy(z, z + 1, 1).wait_send()

    @pl.when(mid)
    def _():
        for k in range(1, ZED):
            fwd_copy(k).wait_send()
    for k in range(ZED):
        for o in order:
            d_copy(k, o).wait_send()
            b_copy(k, o).wait_send()
    for k in range(1, ZED):
        for s in range(SLICES):
            s_copy(k, s).wait_send()


def split_gates(gates):
    first = lax.reduce_precision(gates, 8, 7)
    second = lax.reduce_precision(gates - first, 8, 7)
    third = gates - first - second
    return first, second, third


def solution(mesh):
    ep_axes = tuple(mesh.axis_names)
    num_devices = math.prod(mesh.shape[a] for a in ep_axes)
    row_spec = P(ep_axes, None)
    w_spec = P(ep_axes, None, None)

    def local_layer(tokens, expert_ids, gate_weights, w_gate, w_up, w_down):
        tok, wide = tokens.shape
        ff = w_gate.shape[2]
        cap = tok * expert_ids.shape[1] // num_devices
        rows = PLANE * cap
        ft, nt = 256, 256
        full = wide + TAIL

        def eight(v):
            return jnp.pad(v.astype(F32), ((0, 0), (0, 2)), constant_values=-1.0)
        parts = [eight(expert_ids // 2), eight(expert_ids)]
        parts += [eight(g) for g in split_gates(gate_weights)]
        tail = jnp.concatenate(parts, axis=1)
        tail = jnp.pad(tail, ((0, 0), (0, TAIL - tail.shape[1]))).astype(BF)

        dims = (tok, wide, ff, cap, ft, nt)
        vm = pl.BlockSpec(memory_space=pltpu.VMEM)
        hbm = pl.BlockSpec(memory_space=pl.ANY)
        dma = pltpu.SemaphoreType.DMA
        return pl.pallas_call(
            functools.partial(layer_kernel, dims),
            out_shape=jax.ShapeDtypeStruct((tok, wide), BF),
            in_specs=[hbm, vm, hbm, hbm, hbm],
            out_specs=vm,
            scratch_shapes=[
                pltpu.VMEM((ZED, tok, full), BF),
                pltpu.VMEM((ZED, rows, full), BF),
                pltpu.VMEM((ZED, rows, full), BF),
                pltpu.VMEM((ZED, rows, wide), BF),
                pltpu.VMEM((2, rows, ff), BF),
                pltpu.VMEM((ZED - 1, tok, wide), BF),
                pltpu.VMEM((ZED + 1, tok, wide), BF),
                pltpu.VMEM((ZED, tok, rows), BF),
                pltpu.VMEM((2, 2, wide, ft), BF),
                pltpu.VMEM((2, 2, ff, nt), BF),
                dma((1,)), dma((2, 2)), dma((2, 2)),
                dma((5,)), dma((ZED,)),
                dma((ZED, PLANE)), dma((ZED, PLANE)),
                dma((ZED, PLANE)), dma((ZED, PLANE)),
                dma((ZED - 1, SLICES)), dma((ZED + 1, SLICES)),
            ],
            compiler_params=pltpu.CompilerParams(
                collective_id=0, has_side_effects=True, vmem_limit_bytes=67_000_000),
            name="moe_layer",
        )(tokens, tail, w_gate, w_up, w_down)

    return jax.shard_map(local_layer, mesh=mesh, in_specs=(row_spec, row_spec, row_spec, w_spec, w_spec, w_spec), out_specs=row_spec, check_vma=False)
```

time: 500 us -> 270 us (0.54)
  Pallas kernels: 0 us -> 263 us
  blocking collectives: 187 us -> 0 us
  waiting for transfers between devices: 138 us -> 0 us
  matrix products: 69.2 us -> 0 us
  other arithmetic: 46.1 us -> 1.49 us
  local copies, waits for them, and re-layouts: 45.5 us -> 3.26 us
  starting transfers between devices: 12.9 us -> 0 us
    pallas_call x0 -> x1, Pallas kernels: none -> 263 us  [local_layer(): pl.pallas_call(functools.partial(layer_kernel, dims), out_shape=jax.Shape...]
    all_to_all x1 -> x0, blocking collectives: 187 us -> none  [local_layer(): returned = lax.all_to_all(back_rows, ep_axes, 0, 0, tiled=True)]
    all_to_all x2 -> x0, waiting for transfers between devices: 138 us -> none  [the longest x1 138 us: local_layer(): recv_rows = lax.all_to_all(send_rows, ep_axes, 0, 0, tiled=True)]
    dot_general x5 -> x0, matrix products: 69.2 us -> none  [the longest x1 20.5 us: expert_ffn(): jnp.einsum('lcf,lfh->lch', hidden_act, w_down, preferred_element_type=jnp...]
    scatter-add x1 -> x0, other arithmetic: 31.7 us -> none  [local_layer(): jax.ops.segment_sum(weighted.reshape(-1, hidden), pick_rows.reshape(-1),...]
    gather x1 -> x0, local copies, waits for them, and re-layouts: 19.5 us -> none  [local_layer(): flat_rows[pick_rows]]
    all_to_all x2 -> x0, starting transfers between devices: 12.9 us -> none  [the longest x1 7.36 us: local_layer(): recv_gates = lax.all_to_all(send_gates, ep_axes, 0, 0, tiled=True)]
    another operation x4 -> x0, local copies, waits for them, and re-layouts: 12 us -> none  [the longest x1 11.8 us: local_layer(): jax.ops.segment_sum(weighted.reshape(-1, hidden), pick_rows.reshape(-1),...]
  transfers between devices with their start and end apart: 2 -> 0, of which waited for: 2 -> 0; matrix products, arithmetic and copies ran while one was open for 7% -> 0% of each run, Pallas kernels for 0% -> 0%
where the time goes in v1:
time: 270 us; the launch traced here: 268 us
  Pallas kernels  263 us (97%)
  local copies, waits for them, and re-layouts  3.26 us (1%)
    pallas_call x1, Pallas kernels, local_layer(): pl.pallas_call(functools.partial(layer_kernel, dims), out_shape=jax.Shape...  263 us

profile of v1, /device:TPU:0, one launch (start us, length us, event | category | flops | bytes accessed | tf_op | source)
XLA Modules:
  0.0 267.8 jit_solution(17706446458265597071)
XLA Ops:
  0.0 0.8 convert_convert_fusion
  0.8 0.7 fusion
  1.5 0.1 copy.14
  1.7 0.7 pad.31.tail_ref
  2.3 263.0 %moe_layer.1 = bf16[256,2560]{1,0:T(8,128)(2,1)} custom-call(bf16[256,2560]{1,0:T(8,128)(2,1)} %x_ref.1, bf16[256,128]{1,0:T(8,128)(2,1)} %pad.31.tail_ref, bf16[2,2560,1536]{2,1,0:T(8,128)(2,1)} %w1_ref.1, bf16[2,2560,1536]{2,1,0:T(8,128)(2,1)} %w3_ref.1, bf16[2,1536,2560]{2,1,0:T(8,128)(2,1)} %w2_ref.1), custom_call_target="tpu_custom_call" | custom-call | tf_op jit(solution)/shard_map/moe_layer/pallas_call | solution.py:410
  265.3 2.5 copy.20
  (5 shorter events, 0.0 us)

commit v2 on v1

--- a/solution.py
+++ b/solution.py
@@ -14,16 +14,21 @@
 PLANE = 8
 ZED = 4
 SLICES = 4
+HALVES = 2
+FT = 512
+NT = 512
 
 
 def layer_kernel(dims, x_ref, tail_ref, w1_ref, w3_ref, w2_ref, y_ref,
-                 zbuf, send, recv, back, hid, zsend, zrecv, unpack, wa, wb,
+                 zbuf, send, recv, back, hid, gate, zsend, zrecv, unpack, wa, wb,
                  x_sem, wa_sem, wb_sem, z_ssem, z_rsem, d_ssem, d_rsem,
                  b_ssem, b_rsem, s_ssem, s_rsem):
     tok, wide, ff, cap, ft, nt = dims
     rows = PLANE * cap
     full = wide + TAIL
     sw = wide // SLICES
+    hw = wide // HALVES
+    per_half = SLICES // HALVES
     n_f, n_n = ff // ft, wide // nt
     z = lax.axis_index("ez")
     ey = lax.axis_index("ey")
@@ -148,10 +153,6 @@
             d_copy(k, o).start()
         recv[k, rows_of(me), :] = send[k, rows_of(me), :]
 
-    def service(k):
-        z_wait(k)
-        relay(k)
-
     def forward(k):
         @pl.when(mid)
         def _():
@@ -161,71 +162,70 @@
         for o in order:
             d_copy(k, o).wait_recv()
 
-    def stage_a(k, l):
-        def step(i, carry):
-            @pl.when(i + 1 < 2 * n_f)
-            def _():
-                for c in a_copies(i + 1):
-                    c.start()
-
-            @pl.when(i + 1 == 2 * n_f)
-            def _():
-                for c in b_copies(0):
-                    c.start()
-            for c in a_copies(i):
-                c.wait()
-            slot = i % 2
-            x = recv[k, :, :wide]
-            a = jnp.dot(x, wa[slot, 0], preferred_element_type=F32)
-            b = jnp.dot(x, wa[slot, 1], preferred_element_type=F32)
-            cols = pl.ds(pl.multiple_of((i - l * n_f) * ft, ft), ft)
-            hid[l, :, cols] = (jax.nn.silu(a) * b).astype(BF)
-            return carry
-        lax.fori_loop(l * n_f, (l + 1) * n_f, step, 0)
-
-    def stage_b(k):
+    def step_a(k, i):
+        @pl.when(i + 1 < 2 * n_f)
+        def _():
+            for c in a_copies(i + 1):
+                c.start()
+
+        @pl.when(i + 1 == 2 * n_f)
+        def _():
+            for c in b_copies(0):
+                c.start()
+        for c in a_copies(i):
+            c.wait()
+        slot = i % 2
+        x = recv[k, :, :wide]
+        a = jnp.dot(x, wa[slot, 0], preferred_element_type=F32)
+        b = jnp.dot(x, wa[slot, 1], preferred_element_type=F32)
+        cols = pl.ds(pl.multiple_of((i % n_f) * ft, ft), ft)
+        hid[i // n_f, :, cols] = (jax.nn.silu(a) * b).astype(BF)
+
+    def step_gate(k):
         tail = recv[k, :, wide:].astype(F32)
         lane = lax.broadcasted_iota(jnp.int32, (rows, TAIL), 1)
-        gate = []
         for l in range(2):
             at = jnp.where(lane < 48, jnp.bitwise_and(lane, 15), -1) == me * 2 + l
-            gate.append(jnp.sum(jnp.where(at, tail, 0.0), axis=1, keepdims=True))
-
-        def step(n, carry):
-            @pl.when(n + 1 < n_n)
-            def _():
-                for c in b_copies(n + 1):
-                    c.start()
-            if k < ZED - 1:
-                @pl.when(n + 1 == n_n)
-                def _():
-                    for c in a_copies(0):
-                        c.start()
-            for c in b_copies(n):
-                c.wait()
-            slot = n % 2
-            o0 = jnp.dot(hid[0], wb[slot, 0], preferred_element_type=F32)
-            o1 = jnp.dot(hid[1], wb[slot, 1], preferred_element_type=F32)
-            cols = pl.ds(pl.multiple_of(n * nt, nt), nt)
-            recv[k, :, cols] = (gate[0] * o0 + gate[1] * o1).astype(BF)
-            return carry
-        lax.fori_loop(0, n_n, step, 0)
-
-    def b_copy(k, o):
+            g = jnp.sum(jnp.where(at, tail, 0.0), axis=1, keepdims=True)
+            gate[l] = jnp.broadcast_to(g, (rows, TAIL))
+
+    def step_b(k, n):
+        @pl.when(n + 1 < n_n)
+        def _():
+            for c in b_copies(n + 1):
+                c.start()
+
+        @pl.when(jnp.logical_and(n + 1 == n_n, k < ZED - 1))
+        def _():
+            for c in a_copies(0):
+                c.start()
+        for c in b_copies(n):
+            c.wait()
+        slot = n % 2
+        o0 = jnp.dot(hid[0], wb[slot, 0], preferred_element_type=F32)
+        o1 = jnp.dot(hid[1], wb[slot, 1], preferred_element_type=F32)
+        g0 = jnp.concatenate([gate[0]] * (nt // TAIL), axis=1)
+        g1 = jnp.concatenate([gate[1]] * (nt // TAIL), axis=1)
+        cols = pl.ds(pl.multiple_of(n * nt, nt), nt)
+        recv[k, :, cols] = (g0 * o0 + g1 * o1).astype(BF)
+
+    def b_copy(k, h, o):
         cy, cx = peer(o)
+        cols = pl.ds(h * hw, hw)
         return pltpu.make_async_remote_copy(
-            src_ref=recv.at[k, rows_of(cy * 4 + cx), pl.ds(0, wide)], dst_ref=back.at[k, rows_of(me)],
-            send_sem=b_ssem.at[k, o], recv_sem=b_rsem.at[k, o],
+            src_ref=recv.at[k, rows_of(cy * 4 + cx), cols], dst_ref=back.at[k, rows_of(me), cols],
+            send_sem=b_ssem.at[k, h, o], recv_sem=b_rsem.at[k, h, o],
             device_id=(z, cy, cx), device_id_type=MESH)
 
-    def give_back(k):
+    def give_back(k, h):
         for o in order:
-            b_copy(k, o).start()
-        back[k, rows_of(me), :] = recv[k, rows_of(me), :wide]
-
-    def back_wait(k):
+            b_copy(k, h, o).start()
+        cols = slice(h * hw, h * hw + hw)
+        back[k, rows_of(me), cols] = recv[k, rows_of(me), cols]
+
+    def back_wait(k, h):
         for o in order:
-            b_copy(k, o).wait_recv()
+            b_copy(k, h, o).wait_recv()
 
     def s_copy(k, s):
         if k == 1:
@@ -251,108 +251,132 @@
     def partial(k, s):
         return jnp.dot(unpack[k], back[k, :, s * sw:s * sw + sw], preferred_element_type=F32)
 
-    def finish_end(k):
-        for s in range(SLICES):
+    def slices(h):
+        return range(h * per_half, h * per_half + per_half)
+
+    def finish_end(k, h):
+        back_wait(k, h)
+        for s in slices(h):
             zsend[k - 1, :, s * sw:s * sw + sw] = partial(k, s).astype(BF)
             s_copy(k, s).start()
 
-    def finish_mid(k):
-        for s in range(SLICES):
+    def finish_mid(k, h):
+        back_wait(k, h)
+        for s in slices(h):
             cols = slice(s * sw, s * sw + sw)
             s_wait(src_z[k], s)
             total = partial(k, s) + zrecv[src_z[k], :, cols].astype(F32)
             zsend[k - 1, :, cols] = total.astype(BF)
             s_copy(k, s).start()
 
-    def finish(k):
-        back_wait(k)
-        pl.when(end)(lambda: finish_end(k))
-        pl.when(mid)(lambda: finish_mid(k))
+    def finish_home(h):
+        back_wait(0, h)
+        for s in slices(h):
+            cols = slice(s * sw, s * sw + sw)
+
+            @pl.when(z > 0)
+            def _():
+                s_wait(z, s)
+
+            @pl.when(z < 3)
+            def _():
+                s_wait(4, s)
+            total = zbuf[z, :, cols].astype(F32) + partial(0, s)
+
+            @pl.when(z == 0)
+            def _():
+                y_ref[:, cols] = (total + zrecv[4, :, cols].astype(F32)).astype(BF)
+
+            @pl.when(z == 3)
+            def _():
+                y_ref[:, cols] = (total + zrecv[3, :, cols].astype(F32)).astype(BF)
+
+            @pl.when(mid)
+            def _():
+                both = zrecv[z, :, cols].astype(F32) + zrecv[4, :, cols].astype(F32)
+                y_ref[:, cols] = (total + both).astype(BF)
+
+    per = 2 * n_f + n_n
+    third = 2 * n_f + (n_n + 1) // 2
+
+    def mids_take(k):
+        z_wait(k)
+        fwd_copy(k).start()
+
+    def first_arrivals():
+        z_wait(1)
+        forward(1)
+        pl.when(mid)(lambda: mids_take(2))
+        relay(1)
+
+    def end_relay(k):
+        z_wait(k)
+        relay(k)
+
+    every = z >= 0
+    events = (
+        (2, every, first_arrivals),
+        (per - 1, mid, lambda: relay(2)),
+        (per, every, lambda: arrive(1)),
+        (per + 2, end, lambda: end_relay(2)),
+        (per + 2, mid, lambda: mids_take(3)),
+        (per + 4, mid, lambda: relay(3)),
+        (per + third, every, lambda: give_back(1, 0)),
+        (2 * per, every, lambda: arrive(2)),
+        (2 * per + 2, end, lambda: end_relay(3)),
+        (2 * per + 3, every, lambda: give_back(1, 1)),
+        (2 * per + 4, end, lambda: finish_end(1, 0)),
+        (2 * per + third, every, lambda: give_back(2, 0)),
+        (3 * per, mid, lambda: give_back(2, 1)),
+        (3 * per, every, lambda: arrive(3)),
+        (3 * per + 4, end, lambda: finish_end(1, 1)),
+        (3 * per + third - 1, end, lambda: finish_end(2, 0)),
+        (3 * per + third, every, lambda: give_back(3, 0)),
+    )
 
     relay(0)
     arrive(0)
-    stage_a(0, 0)
-    z_wait(1)
-    forward(1)
+
+    def step(t, carry):
+        for when, cond, act in events:
+            pl.when(jnp.logical_and(t == when, cond))(act)
+        k, i = t // per, t % per
+
+        @pl.when(i == 2 * n_f)
+        def _():
+            step_gate(k)
+
+        @pl.when(i < 2 * n_f)
+        def _():
+            step_a(k, i)
+
+        @pl.when(i >= 2 * n_f)
+        def _():
+            step_b(k, i - 2 * n_f)
+        return carry
+    lax.fori_loop(0, ZED * per, step, 0)
+
+    give_back(3, 1)
+    pl.when(end)(lambda: give_back(2, 1))
+    give_back(0, 0)
+    give_back(0, 1)
+
+    @pl.when(end)
+    def _():
+        finish_end(3, 0)
+        finish_end(3, 1)
+        finish_end(2, 1)
 
     @pl.when(mid)
     def _():
-        z_wait(2)
-        fwd_copy(2).start()
-    relay(1)
-    stage_a(0, 1)
-    stage_b(0)
-
-    arrive(1)
-    stage_a(1, 0)
-
-    @pl.when(end)
-    def _():
-        z_wait(2)
-    relay(2)
-
-    @pl.when(mid)
-    def _():
-        z_wait(3)
-        fwd_copy(3).start()
-    stage_a(1, 1)
-    stage_b(1)
-    give_back(1)
-
-    arrive(2)
-    stage_a(2, 0)
-
-    @pl.when(end)
-    def _():
-        z_wait(3)
-    relay(3)
-    stage_a(2, 1)
-    stage_b(2)
-    give_back(2)
-
-    @pl.when(end)
-    def _():
-        back_wait(1)
-        finish_end(1)
-    arrive(3)
-    stage_a(3, 0)
-    stage_a(3, 1)
-    stage_b(3)
-    give_back(3)
-    give_back(0)
-    finish(2)
-    finish(3)
-
-    @pl.when(mid)
-    def _():
-        back_wait(1)
-        finish_mid(1)
-    back_wait(0)
-
-    for s in range(SLICES):
-        cols = slice(s * sw, s * sw + sw)
-
-        @pl.when(z > 0)
-        def _():
-            s_wait(z, s)
-
-        @pl.when(z < 3)
-        def _():
-            s_wait(4, s)
-        total = zbuf[z, :, cols].astype(F32) + partial(0, s)
-
-        @pl.when(z == 0)
-        def _():
-            y_ref[:, cols] = (total + zrecv[4, :, cols].astype(F32)).astype(BF)
-
-        @pl.when(z == 3)
-        def _():
-            y_ref[:, cols] = (total + zrecv[3, :, cols].astype(F32)).astype(BF)
-
-        @pl.when(mid)
-        def _():
-            both = zrecv[z, :, cols].astype(F32) + zrecv[4, :, cols].astype(F32)
-            y_ref[:, cols] = (total + both).astype(BF)
+        finish_mid(2, 0)
+        finish_mid(3, 0)
+        finish_mid(1, 0)
+        finish_mid(3, 1)
+        finish_mid(1, 1)
+        finish_mid(2, 1)
+    for h in range(HALVES):
+        finish_home(h)
 
     @pl.when(z > 0)
     def _():
@@ -369,7 +393,8 @@
     for k in range(ZED):
         for o in order:
             d_copy(k, o).wait_send()
-            b_copy(k, o).wait_send()
+            for h in range(HALVES):
+                b_copy(k, h, o).wait_send()
     for k in range(1, ZED):
         for s in range(SLICES):
             s_copy(k, s).wait_send()
@@ -393,7 +418,7 @@
         ff = w_gate.shape[2]
         cap = tok * expert_ids.shape[1] // num_devices
         rows = PLANE * cap
-        ft, nt = 256, 256
+        ft, nt = FT, NT
         full = wide + TAIL
 
         def eight(v):
@@ -418,6 +443,7 @@
                 pltpu.VMEM((ZED, rows, full), BF),
                 pltpu.VMEM((ZED, rows, wide), BF),
                 pltpu.VMEM((2, rows, ff), BF),
+                pltpu.VMEM((2, rows, TAIL), F32),
                 pltpu.VMEM((ZED - 1, tok, wide), BF),
                 pltpu.VMEM((ZED + 1, tok, wide), BF),
                 pltpu.VMEM((ZED, tok, rows), BF),
@@ -426,7 +452,7 @@
                 dma((1,)), dma((2, 2)), dma((2, 2)),
                 dma((5,)), dma((ZED,)),
                 dma((ZED, PLANE)), dma((ZED, PLANE)),
-                dma((ZED, PLANE)), dma((ZED, PLANE)),
+                dma((ZED, HALVES, PLANE)), dma((ZED, HALVES, PLANE)),
                 dma((ZED - 1, SLICES)), dma((ZED + 1, SLICES)),
             ],
             compiler_params=pltpu.CompilerParams(

time: 270 us -> 229 us (0.85)
  the two profiles are of different devices: /device:TPU:0 before, /device:TPU:10 now
where the time goes in v2:
time: 229 us
  Pallas kernels  224 us (98%)
  local copies, waits for them, and re-layouts  3.26 us (1%)
    pallas_call x1, Pallas kernels, local_layer(): pl.pallas_call(functools.partial(layer_kernel, dims), out_shape=jax.Shape...  224 us

profile of v2, /device:TPU:10, one launch (start us, length us, event | category | flops | bytes accessed | tf_op | source)
XLA Modules:
  0.0 228.7 jit_solution(11637119454074469664)
XLA Ops:
  0.0 0.8 convert_convert_fusion
  0.8 0.7 fusion
  1.5 0.1 copy.14
  1.7 0.7 pad.31.tail_ref
  2.3 223.9 %moe_layer.1 = bf16[256,2560]{1,0:T(8,128)(2,1)} custom-call(bf16[256,2560]{1,0:T(8,128)(2,1)} %x_ref.1, bf16[256,128]{1,0:T(8,128)(2,1)} %pad.31.tail_ref, bf16[2,2560,1536]{2,1,0:T(8,128)(2,1)} %w1_ref.1, bf16[2,2560,1536]{2,1,0:T(8,128)(2,1)} %w3_ref.1, bf16[2,1536,2560]{2,1,0:T(8,128)(2,1)} %w2_ref.1), custom_call_target="tpu_custom_call" | custom-call | tf_op jit(solution)/shard_map/moe_layer/pallas_call | solution.py:435
  226.3 2.5 %copy.20 = bf16[256,2560]{1,0:T(8,128)(2,1)} copy(bf16[256,2560]{1,0:T(8,128)(2,1)} %moe_layer.1) | data formatting | bytes 2621440
  (5 shorter events, 0.0 us)

commit v3 on v2

v3 whole, which is shorter than its diff:
```python
import functools
import math
import jax
import jax.numpy as jnp
from jax import lax
from jax.experimental import pallas as pl
from jax.experimental.pallas import tpu as pltpu
from jax.sharding import PartitionSpec as P

BF = jnp.bfloat16
F32 = jnp.float32
MESH = pl.DeviceIdType.MESH
TAIL = 128
PLANE = 8
ZED = 4
SLICES = 10
HALVES = 2
FIRST = 6
EARLY = 3
FT = 512
NT = 512


def layer_kernel(dims, x_ref, ids_ref, g_ref, w1_ref, w3_ref, w2_ref, y_ref,
                 zbuf, send, recv, back, hid, gate, zsend, zrecv, unpack, pick, meta, y_buf, wa, wb,
                 x_sem, y_sem, wa_sem, wb_sem, z_ssem, z_rsem, d_ssem, d_rsem,
                 b_ssem, b_rsem, s_ssem, s_rsem):
    tok, wide, ff, cap, ft, nt = dims
    rows = PLANE * cap
    full = wide + TAIL
    sw = wide // SLICES
    starts = (0, FIRST * sw, wide)
    n_f, n_n = ff // ft, wide // nt
    z = lax.axis_index("ez")
    ey = lax.axis_index("ey")
    ex = lax.axis_index("ex")
    me = ey * 4 + ex
    mid = jnp.logical_and(z > 0, z < 3)
    end = jnp.logical_or(z < 1, z > 2)

    def peer(o):
        cy = ey if o < 4 else 1 - ey
        cx = (ex, ex + 1 - 2 * (ex % 2), (ex + 2) % 4, 3 - ex)[o % 4]
        return cy, cx

    def rows_of(q):
        return pl.ds(pl.multiple_of(q * cap, cap), cap)

    src_z = (z, z + 1 - 2 * (z % 2), 2 - z // 2, 3 - 3 * (z // 2))
    order = (6, 4, 2, 7, 5, 3, 1)
    others = pl.ds(0, (PLANE - 1) * cap)

    def slices(h, k=0):
        cut = EARLY if k == 1 else FIRST
        return range(0, cut) if h == 0 else range(cut, SLICES)

    def hidden(h, off=0):
        return pl.ds(off + starts[h], starts[h + 1] - starts[h])

    def half(h):
        return pl.ds(0, TAIL + starts[1]) if h == 0 else hidden(1, TAIL)

    barrier = pltpu.get_barrier_semaphore()
    for o in range(1, PLANE):
        cy, cx = peer(o)
        pl.semaphore_signal(barrier, inc=1, device_id=(z, cy, cx), device_id_type=MESH)

    @pl.when(z > 0)
    def _():
        pl.semaphore_signal(barrier, inc=1, device_id=(z - 1, ey, ex), device_id_type=MESH)

    @pl.when(z < 3)
    def _():
        pl.semaphore_signal(barrier, inc=1, device_id=(z + 1, ey, ex), device_id_type=MESH)

    own = pltpu.make_async_copy(x_ref, zbuf.at[z, :, pl.ds(TAIL, wide)], x_sem.at[0])
    own.start()
    ids = ids_ref[...]
    top_k = ids.shape[0]
    first = g_ref[...].astype(BF).astype(F32)
    rest = g_ref[...] - first
    second = rest.astype(BF).astype(F32)
    meta[...] = jnp.zeros_like(meta)
    terms = (lax.shift_right_logical(ids, 1).astype(F32), ids.astype(F32), first, second, rest - second)
    for n, term in enumerate(terms):
        meta[8 * n:8 * n + top_k, :] = term
    zbuf[z, :, :TAIL] = jnp.transpose(meta[...]).astype(BF)

    def a_copies(i):
        l, f, slot = i // n_f, i % n_f, i % 2
        cols = pl.ds(pl.multiple_of(f * ft, ft), ft)
        return [pltpu.make_async_copy(w.at[l, :, cols], wa.at[slot, j], wa_sem.at[slot, j])
                for j, w in enumerate((w1_ref, w3_ref))]

    def b_copies(n):
        slot = n % 2
        cols = pl.ds(pl.multiple_of(n * nt, nt), nt)
        return [pltpu.make_async_copy(w2_ref.at[l, :, cols], wb.at[slot, l], wb_sem.at[slot, l])
                for l in range(2)]

    own.wait()
    pl.semaphore_wait(barrier, PLANE - 1 + jnp.where(mid, 2, 1))

    def z_copy(block, target, i, h):
        return pltpu.make_async_remote_copy(
            src_ref=zbuf.at[block, :, half(h)], dst_ref=zbuf.at[block, :, half(h)],
            send_sem=z_ssem.at[i, h], recv_sem=z_rsem.at[block, h],
            device_id=(target, ey, ex), device_id_type=MESH)

    @pl.when(z > 0)
    def _():
        for h in range(HALVES):
            z_copy(z, z - 1, 0, h).start()

    @pl.when(z < 3)
    def _():
        for h in range(HALVES):
            z_copy(z, z + 1, 1, h).start()

    for c in a_copies(0):
        c.start()

    def fwd_copy(k, h):
        return z_copy(src_z[k], 3 - z if k == 1 else 3 * (z - 1), 1 + k, h)

    def z_wait(k, h):
        z_copy(src_z[k], z, 0, h).wait_recv()

    def d_copy(k, h, o):
        cy, cx = peer(o)
        return pltpu.make_async_remote_copy(
            src_ref=send.at[k, rows_of(cy * 4 + cx), half(h)], dst_ref=recv.at[k, rows_of(me), half(h)],
            send_sem=d_ssem.at[k], recv_sem=d_rsem.at[k, h],
            device_id=(z, cy, cx), device_id_type=MESH)

    def route(k):
        b = src_z[k]
        tail = zbuf[b, :, :TAIL].astype(F32)
        lane = lax.broadcasted_iota(jnp.int32, (tok, TAIL), 1)
        want_dev = jnp.where(lane < PLANE, z * PLANE + lane, -2).astype(F32)
        want_exp = jnp.where(lane < 48, z * 16 + jnp.bitwise_and(lane, 15), -2).astype(F32)
        hit = jnp.zeros((tok, TAIL), F32)
        gates = jnp.zeros((tok, TAIL), F32)
        for j in range(6):
            hit = jnp.where(tail[:, j:j + 1] == want_dev, 1.0, hit)
            part = jnp.where(lane < 16, tail[:, 16 + j:17 + j],
                             jnp.where(lane < 32, tail[:, 24 + j:25 + j], tail[:, 32 + j:33 + j]))
            gates = jnp.where(tail[:, 8 + j:9 + j] == want_exp, part, gates)
        r_i = lax.broadcasted_iota(jnp.int32, (tok, tok), 0)
        c_i = lax.broadcasted_iota(jnp.int32, (tok, tok), 1)
        tri = jnp.where(c_i <= r_i, 1.0, 0.0).astype(BF)
        rank = jnp.dot(tri, hit.astype(BF), preferred_element_type=F32)
        pos = jnp.where(hit > 0.0, rank, 0.0).astype(BF)
        d_i = lax.broadcasted_iota(jnp.int32, (TAIL, rows), 0)
        s_i = lax.broadcasted_iota(jnp.int32, (TAIL, rows), 1)
        spread = jnp.where(jnp.logical_and(s_i >= d_i * cap, s_i < d_i * cap + cap), 1.0, 0.0).astype(BF)
        l_i = lax.broadcasted_iota(jnp.int32, (tok, rows), 1)
        slot_l = l_i + 1
        for q in range(1, PLANE):
            slot_l = slot_l - jnp.where(l_i >= q * cap, cap, 0)
        at_l = jnp.dot(pos, spread, preferred_element_type=F32)
        unpack[k] = jnp.where(at_l == slot_l.astype(F32), 1.0, 0.0).astype(BF)
        d_t = lax.broadcasted_iota(jnp.int32, (rows, TAIL), 1)
        s_t = lax.broadcasted_iota(jnp.int32, (rows, TAIL), 0)
        spread_t = jnp.where(jnp.logical_and(s_t >= d_t * cap, s_t < d_t * cap + cap), 1.0, 0.0).astype(BF)
        r_t = lax.broadcasted_iota(jnp.int32, (rows, tok), 0)
        slot_r = r_t + 1
        for q in range(1, PLANE):
            slot_r = slot_r - jnp.where(r_t >= q * cap, cap, 0)
        at_r = lax.dot_general(spread_t, pos, (((1,), (1,)), ((), ())), preferred_element_type=F32)
        pick[...] = jnp.where(at_r == slot_r.astype(F32), 1.0, 0.0).astype(BF)
        send[k, :, :TAIL] = jnp.dot(pick[...], gates.astype(BF), preferred_element_type=F32).astype(BF)

    def relay(k, h):
        if h == 0:
            route(k)
        for s in slices(h):
            cols = slice(TAIL + s * sw, TAIL + s * sw + sw)
            send[k, :, cols] = jnp.dot(pick[...], zbuf[src_z[k], :, cols], preferred_element_type=F32).astype(BF)
        for o in order:
            d_copy(k, h, o).start()
        recv[k, rows_of(me), half(h)] = send[k, rows_of(me), half(h)]

    def arrive(k):
        for h in range(HALVES):
            pltpu.make_async_remote_copy(
                src_ref=send.at[k, others, half(h)], dst_ref=recv.at[k, others, half(h)],
                send_sem=d_ssem.at[k], recv_sem=d_rsem.at[k, h],
                device_id=(z, ey, ex), device_id_type=MESH).wait_recv()

    def step_a(k, i):
        @pl.when(i + 1 < 2 * n_f)
        def _():
            for c in a_copies(i + 1):
                c.start()

        @pl.when(i + 1 == 2 * n_f)
        def _():
            for c in b_copies(0):
                c.start()
        for c in a_copies(i):
            c.wait()
        slot = i % 2
        x = recv[k, :, TAIL:]
        a = jnp.dot(x, wa[slot, 0], preferred_element_type=F32)
        b = jnp.dot(x, wa[slot, 1], preferred_element_type=F32)
        cols = pl.ds(pl.multiple_of((i % n_f) * ft, ft), ft)
        hid[i // n_f, :, cols] = (jax.nn.silu(a) * b).astype(BF)

    def step_gate(k):
        tail = recv[k, :, :TAIL].astype(F32)
        lane = lax.broadcasted_iota(jnp.int32, (rows, TAIL), 1)
        for l in range(2):
            at = jnp.where(lane < 48, jnp.bitwise_and(lane, 15), -1) == me * 2 + l
            g = jnp.sum(jnp.where(at, tail, 0.0), axis=1, keepdims=True)
            gate[l] = jnp.broadcast_to(g, (rows, TAIL))

    def step_b(k, n):
        @pl.when(n + 1 < n_n)
        def _():
            for c in b_copies(n + 1):
                c.start()

        @pl.when(jnp.logical_and(n + 1 == n_n, k < ZED - 1))
        def _():
            for c in a_copies(0):
                c.start()
        for c in b_copies(n):
            c.wait()
        slot = n % 2
        o0 = jnp.dot(hid[0], wb[slot, 0], preferred_element_type=F32)
        o1 = jnp.dot(hid[1], wb[slot, 1], preferred_element_type=F32)
        g0 = jnp.concatenate([gate[0]] * (nt // TAIL), axis=1)
        g1 = jnp.concatenate([gate[1]] * (nt // TAIL), axis=1)
        cols = pl.ds(pl.multiple_of(TAIL + n * nt, TAIL), nt)
        recv[k, :, cols] = (g0 * o0 + g1 * o1).astype(BF)

    def back_cols(k, h, off=0):
        part = slices(h, k)
        return pl.ds(off + part[0] * sw, len(part) * sw)

    def b_copy(k, h, rows_there, rows_here, device):
        return pltpu.make_async_remote_copy(
            src_ref=recv.at[k, rows_there, back_cols(k, h, TAIL)], dst_ref=back.at[k, rows_here, back_cols(k, h)],
            send_sem=b_ssem.at[k], recv_sem=b_rsem.at[k, h],
            device_id=device, device_id_type=MESH)

    def give_back(k, h, peers=order):
        for o in peers:
            cy, cx = peer(o)
            b_copy(k, h, rows_of(cy * 4 + cx), rows_of(me), (z, cy, cx)).start()
        if order[-1] in peers:
            back[k, rows_of(me), back_cols(k, h)] = recv[k, rows_of(me), back_cols(k, h, TAIL)]

    def back_wait(k, h):
        b_copy(k, h, others, others, (z, ey, ex)).wait_recv()

    def s_copy(k, s):
        if k == 1:
            target, slot = src_z[1], jnp.where(z % 2 == 0, z + 1, 4)
        elif k == 2:
            target = z + 1 - 2 * (z // 2)
            slot = jnp.where(z < 2, 2, jnp.where(z == 2, 4, 1))
        else:
            target, slot = z + 1 - 2 * (z // 2), src_z[3]
        cols = pl.ds(s * sw, sw)
        return pltpu.make_async_remote_copy(
            src_ref=zsend.at[k - 1, :, cols], dst_ref=zrecv.at[slot, :, cols],
            send_sem=s_ssem.at[k - 1], recv_sem=s_rsem.at[slot, s],
            device_id=(target, ey, ex), device_id_type=MESH)

    def s_wait(slot, s):
        cols = pl.ds(s * sw, sw)
        pltpu.make_async_remote_copy(
            src_ref=zsend.at[0, :, cols], dst_ref=zrecv.at[slot, :, cols],
            send_sem=s_ssem.at[0], recv_sem=s_rsem.at[slot, s],
            device_id=(z, ey, ex), device_id_type=MESH).wait_recv()

    def partial(k, s):
        return jnp.dot(unpack[k], back[k, :, s * sw:s * sw + sw], preferred_element_type=F32)

    def finish_end(k, some):
        for s in some:
            zsend[k - 1, :, s * sw:s * sw + sw] = partial(k, s).astype(BF)
            s_copy(k, s).start()

    def finish_mid(k, some):
        for s in some:
            cols = slice(s * sw, s * sw + sw)
            s_wait(src_z[k], s)
            total = partial(k, s) + zrecv[src_z[k], :, cols].astype(F32)
            zsend[k - 1, :, cols] = total.astype(BF)
            s_copy(k, s).start()

    def y_copy(s):
        cols = pl.ds(s * sw, sw)
        return pltpu.make_async_copy(y_buf.at[:, cols], y_ref.at[:, cols], y_sem.at[0])

    def finish_home(h):
        back_wait(0, h)
        for s in slices(h):
            cols = slice(s * sw, s * sw + sw)

            @pl.when(z > 0)
            def _():
                s_wait(z, s)

            @pl.when(z < 3)
            def _():
                s_wait(4, s)
            x = zbuf[z, :, TAIL + s * sw:TAIL + s * sw + sw].astype(F32)
            total = x + partial(0, s)

            @pl.when(z == 0)
            def _():
                y_buf[:, cols] = (total + zrecv[4, :, cols].astype(F32)).astype(BF)

            @pl.when(z == 3)
            def _():
                y_buf[:, cols] = (total + zrecv[3, :, cols].astype(F32)).astype(BF)

            @pl.when(mid)
            def _():
                both = zrecv[z, :, cols].astype(F32) + zrecv[4, :, cols].astype(F32)
                y_buf[:, cols] = (total + both).astype(BF)
            y_copy(s).start()

    per = 2 * n_f + n_n
    third = 2 * n_f + (n_n + 1) // 2

    def take(k, h):
        z_wait(k, h)
        fwd_copy(k, h).start()

    def mids_take(*which):
        @pl.when(mid)
        def _():
            for k, h in which:
                take(k, h)

    def ends_take(k, h):
        pl.when(end)(lambda: z_wait(k, h))

    def at_start():
        relay(0, 0)
        relay(0, 1)
        ends_take(1, 0)
        mids_take((1, 0), (2, 0))
        relay(1, 0)
        arrive(0)

    def take_1_1():
        ends_take(1, 1)
        mids_take((1, 1), (2, 1))
        relay(1, 1)

    def take_2_0():
        ends_take(2, 0)
        relay(2, 0)

    def take_2_1():
        ends_take(2, 1)
        relay(2, 1)
        mids_take((3, 1),)

    def take_3(h):
        ends_take(3, h)
        relay(3, h)

    def drain_tokens():
        for h in range(HALVES):
            @pl.when(z > 0)
            def _():
                z_copy(z, z - 1, 0, h).wait_send()

            @pl.when(z < 3)
            def _():
                z_copy(z, z + 1, 1, h).wait_send()

            @pl.when(mid)
            def _():
                for k in range(1, ZED):
                    fwd_copy(k, h).wait_send()
        for k in range(ZED):
            pltpu.make_async_remote_copy(
                src_ref=send.at[k, others], dst_ref=recv.at[k, others],
                send_sem=d_ssem.at[k], recv_sem=d_rsem.at[k, 0],
                device_id=(z, ey, ex), device_id_type=MESH).wait_send()

    def drain_rows(k):
        pltpu.make_async_remote_copy(
            src_ref=recv.at[k, others, pl.ds(TAIL, wide)], dst_ref=back.at[k, others],
            send_sem=b_ssem.at[k], recv_sem=b_rsem.at[k, 0],
            device_id=(z, ey, ex), device_id_type=MESH).wait_send()

    def drain_sums(k):
        pltpu.make_async_remote_copy(
            src_ref=zsend.at[k - 1], dst_ref=zrecv.at[0],
            send_sem=s_ssem.at[k - 1], recv_sem=s_rsem.at[0, 0],
            device_id=(z, ey, ex), device_id_type=MESH).wait_send()

    def sum_end(k, h):
        back_wait(k, h)
        finish_end(k, slices(h, k))

    def sum_mid(k, h):
        back_wait(k, h)
        finish_mid(k, slices(h, k))

    every = z >= 0
    events = (
        (3, every, take_1_1),
        (per - 1, every, lambda: give_back(0, 0, (2, 4))),
        (per, every, take_2_0),
        (per, every, lambda: arrive(1)),
        (per + 1, mid, lambda: mids_take((3, 0))),
        (per + 5, every, take_2_1),
        (per + 8, every, lambda: give_back(1, 0)),
        (2 * per, every, lambda: take_3(0)),
        (2 * per, every, lambda: arrive(2)),
        (2 * per + 2, end, lambda: sum_end(1, 0)),
        (2 * per + 4, every, lambda: take_3(1)),
        (2 * per + third, every, lambda: give_back(2, 0)),
        (3 * per, every, lambda: give_back(2, 1)),
        (3 * per, every, lambda: arrive(3)),
        (3 * per + 5, end, lambda: sum_end(2, 0)),
        (3 * per + third, every, lambda: give_back(3, 0)),
        (3 * per + third, end, lambda: sum_end(2, 1)),
        (3 * per + third + 1, mid, lambda: sum_mid(2, 0)),
    )

    at_start()

    def step(t, carry):
        for when, cond, act in events:
            pl.when(jnp.logical_and(t == when, cond))(act)
        k, i = t // per, t % per

        @pl.when(i == 2 * n_f)
        def _():
            step_gate(k)

        @pl.when(i < 2 * n_f)
        def _():
            step_a(k, i)

        @pl.when(i >= 2 * n_f)
        def _():
            step_b(k, i - 2 * n_f)
        return carry
    lax.fori_loop(0, ZED * per, step, 0)

    give_back(3, 1)
    give_back(1, 1)
    give_back(0, 0, (6, 7, 5, 3, 1))
    give_back(0, 1)
    drain_tokens()

    @pl.when(end)
    def _():
        sum_end(3, 0)
        sum_end(3, 1)
        sum_end(1, 1)

    @pl.when(mid)
    def _():
        sum_mid(2, 1)
        sum_mid(3, 0)
        back_wait(1, 0)
        finish_mid(1, slices(0, 1))
        back_wait(1, 1)
        finish_mid(1, range(EARLY, FIRST))
        sum_mid(3, 1)
        finish_mid(1, slices(1))
    for k in range(1, ZED):
        drain_rows(k)
    finish_home(0)
    finish_home(1)
    drain_rows(0)
    for k in range(1, ZED):
        drain_sums(k)
    pltpu.make_async_copy(y_buf, y_ref, y_sem.at[0]).wait()


def solution(mesh):
    ep_axes = tuple(mesh.axis_names)
    num_devices = math.prod(mesh.shape[a] for a in ep_axes)
    row_spec = P(ep_axes, None)
    w_spec = P(ep_axes, None, None)

    def local_layer(tokens, expert_ids, gate_weights, w_gate, w_up, w_down):
        tok, wide = tokens.shape
        ff = w_gate.shape[2]
        cap = tok * expert_ids.shape[1] // num_devices
        rows = PLANE * cap
        ft, nt = FT, NT
        full = wide + TAIL
        dims = (tok, wide, ff, cap, ft, nt)
        vm = pl.BlockSpec(memory_space=pltpu.VMEM)
        hbm = pl.BlockSpec(memory_space=pl.ANY)
        dma = pltpu.SemaphoreType.DMA
        return pl.pallas_call(
            functools.partial(layer_kernel, dims),
            out_shape=jax.ShapeDtypeStruct((tok, wide), BF),
            in_specs=[hbm, vm, vm, hbm, hbm, hbm],
            out_specs=hbm,
            scratch_shapes=[
                pltpu.VMEM((ZED, tok, full), BF),
                pltpu.VMEM((ZED, rows, full), BF),
                pltpu.VMEM((ZED, rows, full), BF),
                pltpu.VMEM((ZED, rows, wide), BF),
                pltpu.VMEM((2, rows, ff), BF),
                pltpu.VMEM((2, rows, TAIL), F32),
                pltpu.VMEM((ZED - 1, tok, wide), BF),
                pltpu.VMEM((ZED + 1, tok, wide), BF),
                pltpu.VMEM((ZED, tok, rows), BF),
                pltpu.VMEM((rows, tok), BF),
                pltpu.VMEM((TAIL, tok), F32),
                pltpu.VMEM((tok, wide), BF),
                pltpu.VMEM((2, 2, wide, ft), BF),
                pltpu.VMEM((2, 2, ff, nt), BF),
                dma((1,)), dma((1,)), dma((2, 2)), dma((2, 2)),
                dma((5, HALVES)), dma((ZED, HALVES)),
                dma((ZED,)), dma((ZED, HALVES)),
                dma((ZED,)), dma((ZED, HALVES)),
                dma((ZED - 1,)), dma((ZED + 1, SLICES)),
            ],
            compiler_params=pltpu.CompilerParams(
                collective_id=0, has_side_effects=True, vmem_limit_bytes=67_000_000),
            name="moe_layer",
        )(tokens, expert_ids.T, gate_weights.T, w_gate, w_up, w_down)

    return jax.shard_map(local_layer, mesh=mesh, in_specs=(row_spec, row_spec, row_spec, w_spec, w_spec, w_spec), out_specs=row_spec, check_vma=False)
```

time: 229 us -> 205 us (0.90)
  the two profiles are of different devices: /device:TPU:10 before, /device:TPU:0 now
where the time goes in v3:
time: 205 us
  Pallas kernels  202 us (99%)
  local copies, waits for them, and re-layouts  2.46 us (1%)
    pallas_call x1, Pallas kernels, local_layer(): pl.pallas_call(functools.partial(layer_kernel, dims), out_shape=jax.Shape...  202 us

profile of v3, /device:TPU:0, one launch (start us, length us, event | category | flops | bytes accessed | tf_op | source)
XLA Modules:
  0.0 204.8 jit_solution(4985914326551549565)
XLA Ops:
  0.0 202.4 %moe_layer.1 = bf16[256,2560]{1,0:T(8,128)(2,1)} custom-call(bf16[256,2560]{1,0:T(8,128)(2,1)} %x_ref.1, s32[6,256]{1,0:T(8,128)} %bitcast.2, f32[6,256]{1,0:T(8,128)} %bitcast.3, bf16[2,2560,1536]{2,1,0:T(8,128)(2,1)} %w1_ref.1, bf16[2,2560,1536]{2,1,0:T(8,128)(2,1)} %w3_ref.1, bf16[2,1536,2560]{2,1,0:T(8,128)(2,1)} %w2_ref.1), custom_call_target="tpu_custom_call" | custom-call | tf_op jit(solution)/shard_map/moe_layer/pallas_call | solution.py:502
  202.4 2.5 %copy.8 = bf16[256,2560]{1,0:T(8,128)(2,1)} copy(bf16[256,2560]{1,0:T(8,128)(2,1)} %moe_layer.1) | data formatting | bytes 2621440

commit v4 on v3

--- a/solution.py
+++ b/solution.py
@@ -16,7 +16,8 @@
 SLICES = 10
 HALVES = 2
 FIRST = 6
-EARLY = 3
+LAG = 2
+CUTS = (0, 3, 6, 10)
 FT = 512
 NT = 512
 
@@ -50,9 +51,13 @@
     order = (6, 4, 2, 7, 5, 3, 1)
     others = pl.ds(0, (PLANE - 1) * cap)
 
-    def slices(h, k=0):
-        cut = EARLY if k == 1 else FIRST
-        return range(0, cut) if h == 0 else range(cut, SLICES)
+    def slices(h):
+        return range(0, FIRST) if h == 0 else range(FIRST, SLICES)
+
+    parts = len(CUTS) - 1
+
+    def part(h):
+        return range(CUTS[h], CUTS[h + 1])
 
     def hidden(h, off=0):
         return pl.ds(off + starts[h], starts[h + 1] - starts[h])
@@ -235,13 +240,12 @@
         cols = pl.ds(pl.multiple_of(TAIL + n * nt, TAIL), nt)
         recv[k, :, cols] = (g0 * o0 + g1 * o1).astype(BF)
 
-    def back_cols(k, h, off=0):
-        part = slices(h, k)
-        return pl.ds(off + part[0] * sw, len(part) * sw)
+    def back_cols(h, off=0):
+        return pl.ds(off + CUTS[h] * sw, len(part(h)) * sw)
 
     def b_copy(k, h, rows_there, rows_here, device):
         return pltpu.make_async_remote_copy(
-            src_ref=recv.at[k, rows_there, back_cols(k, h, TAIL)], dst_ref=back.at[k, rows_here, back_cols(k, h)],
+            src_ref=recv.at[k, rows_there, back_cols(h, TAIL)], dst_ref=back.at[k, rows_here, back_cols(h)],
             send_sem=b_ssem.at[k], recv_sem=b_rsem.at[k, h],
             device_id=device, device_id_type=MESH)
 
@@ -250,7 +254,7 @@
             cy, cx = peer(o)
             b_copy(k, h, rows_of(cy * 4 + cx), rows_of(me), (z, cy, cx)).start()
         if order[-1] in peers:
-            back[k, rows_of(me), back_cols(k, h)] = recv[k, rows_of(me), back_cols(k, h, TAIL)]
+            back[k, rows_of(me), back_cols(h)] = recv[k, rows_of(me), back_cols(h, TAIL)]
 
     def back_wait(k, h):
         b_copy(k, h, others, others, (z, ey, ex)).wait_recv()
@@ -298,7 +302,7 @@
 
     def finish_home(h):
         back_wait(0, h)
-        for s in slices(h):
+        for s in part(h):
             cols = slice(s * sw, s * sw + sw)
 
             @pl.when(z > 0)
@@ -401,32 +405,37 @@
 
     def sum_end(k, h):
         back_wait(k, h)
-        finish_end(k, slices(h, k))
+        finish_end(k, part(h))
 
     def sum_mid(k, h):
         back_wait(k, h)
-        finish_mid(k, slices(h, k))
+        finish_mid(k, part(h))
 
     every = z >= 0
     events = (
         (3, every, take_1_1),
         (per - 1, every, lambda: give_back(0, 0, (2, 4))),
+        (per - 1, every, lambda: give_back(0, 1, (2, 4))),
         (per, every, take_2_0),
         (per, every, lambda: arrive(1)),
         (per + 1, mid, lambda: mids_take((3, 0))),
         (per + 5, every, take_2_1),
-        (per + 8, every, lambda: give_back(1, 0)),
-        (2 * per, every, lambda: take_3(0)),
         (2 * per, every, lambda: arrive(2)),
-        (2 * per + 2, end, lambda: sum_end(1, 0)),
-        (2 * per + 4, every, lambda: take_3(1)),
+        (2 * per, every, lambda: give_back(1, 0)),
+        (2 * per + 2, every, lambda: take_3(0)),
+        (2 * per + 3, end, lambda: sum_end(1, 0)),
+        (2 * per + 5, every, lambda: take_3(1)),
         (2 * per + third, every, lambda: give_back(2, 0)),
-        (3 * per, every, lambda: give_back(2, 1)),
+        (2 * per + third + 1, every, lambda: give_back(2, 1)),
         (3 * per, every, lambda: arrive(3)),
-        (3 * per + 5, end, lambda: sum_end(2, 0)),
-        (3 * per + third, every, lambda: give_back(3, 0)),
-        (3 * per + third, end, lambda: sum_end(2, 1)),
-        (3 * per + third + 1, mid, lambda: sum_mid(2, 0)),
+        (3 * per, every, lambda: give_back(2, 2)),
+        (3 * per + 3, end, lambda: sum_end(2, 0)),
+        (3 * per + 6, end, lambda: sum_end(2, 1)),
+        (3 * per + third - 1, every, lambda: give_back(3, 0)),
+        (3 * per + third, every, lambda: give_back(3, 1)),
+        (3 * per + third - 1, mid, lambda: sum_mid(2, 0)),
+        (3 * per + third + 1, end, lambda: sum_end(2, 2)),
+        (3 * per + third + 1, mid, lambda: sum_mid(2, 1)),
     )
 
     at_start()
@@ -450,32 +459,46 @@
         return carry
     lax.fori_loop(0, ZED * per, step, 0)
 
-    give_back(3, 1)
-    give_back(1, 1)
+    @pl.when(end)
+    def _():
+        give_back(3, 2)
+        give_back(1, 1)
+        give_back(1, 2)
+
+    @pl.when(mid)
+    def _():
+        give_back(1, 1)
+        give_back(3, 2)
+        give_back(1, 2)
     give_back(0, 0, (6, 7, 5, 3, 1))
-    give_back(0, 1)
+    give_back(0, 1, (6, 7, 5, 3, 1))
+    give_back(0, 2)
     drain_tokens()
 
     @pl.when(end)
     def _():
-        sum_end(3, 0)
-        sum_end(3, 1)
-        sum_end(1, 1)
+        for h in range(parts):
+            sum_end(3, h)
+        for h in range(1, parts):
+            sum_end(1, h)
 
     @pl.when(mid)
     def _():
-        sum_mid(2, 1)
-        sum_mid(3, 0)
-        back_wait(1, 0)
-        finish_mid(1, slices(0, 1))
-        back_wait(1, 1)
-        finish_mid(1, range(EARLY, FIRST))
-        sum_mid(3, 1)
-        finish_mid(1, slices(1))
+        sum_mid(2, 2)
+        for s in range(SLICES + LAG):
+            for h in range(parts):
+                if s == CUTS[h]:
+                    back_wait(3, h)
+                if s - LAG == CUTS[h]:
+                    back_wait(1, h)
+            if s < SLICES:
+                finish_mid(3, (s,))
+            if s >= LAG:
+                finish_mid(1, (s - LAG,))
     for k in range(1, ZED):
         drain_rows(k)
-    finish_home(0)
-    finish_home(1)
+    for h in range(parts):
+        finish_home(h)
     drain_rows(0)
     for k in range(1, ZED):
         drain_sums(k)
@@ -522,7 +545,7 @@
                 dma((1,)), dma((1,)), dma((2, 2)), dma((2, 2)),
                 dma((5, HALVES)), dma((ZED, HALVES)),
                 dma((ZED,)), dma((ZED, HALVES)),
-                dma((ZED,)), dma((ZED, HALVES)),
+                dma((ZED,)), dma((ZED, len(CUTS) - 1)),
                 dma((ZED - 1,)), dma((ZED + 1, SLICES)),
             ],
             compiler_params=pltpu.CompilerParams(

time: 205 us -> 200 us (0.976)
  Pallas kernels: 202 us -> 197 us
    pallas_call x1, Pallas kernels: 202 us -> 197 us  [local_layer(): pl.pallas_call(functools.partial(layer_kernel, dims), out_shape=jax.Shape...]
where the time goes in v4:
time: 200 us; the launch traced here: 199 us
  Pallas kernels  197 us (98%)
  local copies, waits for them, and re-layouts  2.46 us (1%)
    pallas_call x1, Pallas kernels, local_layer(): pl.pallas_call(functools.partial(layer_kernel, dims), out_shape=jax.Shape...  197 us

profile of v4, /device:TPU:0, one launch (start us, length us, event | category | flops | bytes accessed | tf_op | source)
XLA Modules:
  0.0 199.2 jit_solution(16501156366853214599)
XLA Ops:
  0.0 196.7 %moe_layer.1 = bf16[256,2560]{1,0:T(8,128)(2,1)} custom-call(bf16[256,2560]{1,0:T(8,128)(2,1)} %x_ref.1, s32[6,256]{1,0:T(8,128)} %bitcast.2, f32[6,256]{1,0:T(8,128)} %bitcast.3, bf16[2,2560,1536]{2,1,0:T(8,128)(2,1)} %w1_ref.1, bf16[2,2560,1536]{2,1,0:T(8,128)(2,1)} %w3_ref.1, bf16[2,1536,2560]{2,1,0:T(8,128)(2,1)} %w2_ref.1), custom_call_target="tpu_custom_call" | custom-call | tf_op jit(solution)/shard_map/moe_layer/pallas_call | solution.py:525
  196.8 2.5 %copy.8 = bf16[256,2560]{1,0:T(8,128)(2,1)} copy(bf16[256,2560]{1,0:T(8,128)(2,1)} %moe_layer.1) | data formatting | bytes 2621440
